TPU v7x, 32 devices: a whole 2x2x4 slice. The times are simulated.
32 devices in a mesh: gx: 4 (over z), gy: 4 (over x, core), gz: 2 (over y).
Axes of the slice: x: 2, y: 2, z: 4, core: 2. Of those that a mesh axis runs over, the one named last changes fastest.
Arguments:
- source: float32 [64, 32, 512], P('gx', 'gz', 'gy'), may hold values from -0.6 to 0.6
- shift: float32 [1], replicated, may hold values from 1e-05 to 0.0001
Outputs:
- solution: float32 [64, 32, 512], P('gx', 'gz', 'gy')
All inputs are finite; a program needn't handle non-finite values.
Results may differ from a plain program's by a relative error of at most 0.0004.
Values sent between devices are 32-bit elements; how exact they have to be, the bound alone decides.
A program may use at most 64 MiB of HBM per device.

v0:
```python
import math

import jax
import jax.numpy as jnp
from jax import lax
from jax.sharding import PartitionSpec as P

LEVELS = 4


DAMPING = 6.0 / 7.0
PRECISE = lax.Precision.HIGHEST
CUBIC_EVEN = (-5.0 / 128.0, 35.0 / 128.0, 105.0 / 128.0, -7.0 / 128.0)
CUBIC_ODD = (-7.0 / 128.0, 105.0 / 128.0, 35.0 / 128.0, -5.0 / 128.0)
LINEAR_EVEN = (0.25, 0.75)
LINEAR_ODD = (0.75, 0.25)


def extended(block, sides, width):
    for axis, dim in sides:
        count = lax.axis_size(axis)
        forward = [(i, i + 1) for i in range(count - 1)]
        forward.append((count - 1, 0))
        backward = [(target, source) for source, target in forward]
        low = lax.ppermute(
            lax.slice_in_dim(block, block.shape[dim] - width, None, axis=dim), axis, forward
        )
        high = lax.ppermute(lax.slice_in_dim(block, 0, width, axis=dim), axis, backward)
        block = jnp.concatenate([low, block, high], axis=dim)
    return block


def wrapped(values, width):
    return jnp.pad(values, width, mode="wrap")


def neighbours(padded):
    center = padded[1:-1, 1:-1, 1:-1]
    beside_all = padded[2:, 1:-1, 1:-1] + padded[:-2, 1:-1, 1:-1]
    beside_all = beside_all + padded[1:-1, 2:, 1:-1] + padded[1:-1, :-2, 1:-1]
    beside_all = beside_all + padded[1:-1, 1:-1, 2:] + padded[1:-1, 1:-1, :-2]
    return (center, beside_all)


def defect(padded, forcing, weight_nb, diagonal):
    center, beside_all = neighbours(padded)
    return forcing - (diagonal * center - weight_nb * beside_all)


def relaxed(padded, forcing, weight_nb, diagonal):
    center, beside_all = neighbours(padded)
    return center + DAMPING * (forcing - (diagonal * center - weight_nb * beside_all)) / diagonal


def coarsen(values):
    values = values[0::2] + values[1::2]
    values = values[:, 0::2] + values[:, 1::2]
    values = values[:, :, 0::2] + values[:, :, 1::2]
    return 0.125 * values


def refine_axis(padded, dimension, even_weights, odd_weights):
    margin = len(even_weights) // 2
    length = padded.shape[dimension] - 2 * margin
    even_cells = even_weights[0] * lax.slice_in_dim(padded, 0, length, axis=dimension)
    odd_cells = odd_weights[0] * lax.slice_in_dim(padded, 1, 1 + length, axis=dimension)
    for offset in range(1, len(even_weights)):
        even_cells = even_cells + even_weights[offset] * lax.slice_in_dim(
            padded, offset, offset + length, axis=dimension
        )
        odd_cells = odd_cells + odd_weights[offset] * lax.slice_in_dim(
            padded, offset + 1, offset + 1 + length, axis=dimension
        )
    stacked = jnp.stack([even_cells, odd_cells], axis=dimension + 1)
    new_shape = list(even_cells.shape)
    new_shape[dimension] = 2 * length
    return stacked.reshape(new_shape)


def refine(padded, even_weights, odd_weights):
    for dimension in range(3):
        padded = refine_axis(padded, dimension, even_weights, odd_weights)
    return padded


def tables(cells_count):
    indices = jnp.arange(cells_count, dtype=jnp.int32)
    angles = (indices[:, None] * indices[None, :] % cells_count).astype(jnp.float32) * (
        2.0 * math.pi / cells_count
    )
    return (jnp.cos(angles), jnp.sin(angles))


def along_axis(matrix, values, dimension):
    product = jnp.tensordot(matrix, values, axes=([1], [dimension]), precision=PRECISE)
    return jnp.moveaxis(product, 0, dimension)


def coarse_solve(forcing, shift_value, weight_nb):
    cosine_table, sine_table = tables(forcing.shape[0])
    real_part = along_axis(cosine_table, forcing, 0)
    imag_part = -along_axis(sine_table, forcing, 0)
    for dimension in (1, 2):
        cosine_table, sine_table = tables(forcing.shape[dimension])
        real_next = along_axis(cosine_table, real_part, dimension) + along_axis(
            sine_table, imag_part, dimension
        )
        imag_part = along_axis(cosine_table, imag_part, dimension) - along_axis(
            sine_table, real_part, dimension
        )
        real_part = real_next
    cosines = [
        jnp.cos(jnp.arange(cells_count, dtype=jnp.float32) * (2.0 * math.pi / cells_count))
        for cells_count in forcing.shape
    ]
    eigenvalue = (
        weight_nb
        * (
            6.0
            - 2.0 * cosines[0][:, None, None]
            - 2.0 * cosines[1][None, :, None]
            - 2.0 * cosines[2][None, None, :]
        )
        + shift_value
    )
    real_part = real_part / eigenvalue
    imag_part = imag_part / eigenvalue
    for dimension in (0, 1):
        cosine_table, sine_table = tables(forcing.shape[dimension])
        real_next = along_axis(cosine_table, real_part, dimension) - along_axis(
            sine_table, imag_part, dimension
        )
        imag_part = along_axis(cosine_table, imag_part, dimension) + along_axis(
            sine_table, real_part, dimension
        )
        real_part = real_next
    cosine_table, sine_table = tables(forcing.shape[2])
    real_part = along_axis(cosine_table, real_part, 2) - along_axis(sine_table, imag_part, 2)
    return real_part / float(forcing.size)


def vcycle_whole(grid_level, iterate, forcing, shift_value):
    weight_nb = 0.25**grid_level
    diagonal = 6.0 * weight_nb + shift_value
    iterate = relaxed(wrapped(iterate, 1), forcing, weight_nb, diagonal)
    residue = coarsen(defect(wrapped(iterate, 1), forcing, weight_nb, diagonal))
    correction = coarse_solve(residue, shift_value, 0.25 ** (grid_level + 1))
    iterate = iterate + refine(wrapped(correction, 1), LINEAR_EVEN, LINEAR_ODD)
    iterate = relaxed(wrapped(iterate, 1), forcing, weight_nb, diagonal)
    return iterate


def collect(block):
    gathered = lax.all_gather(block[None], ("gx", "gy", "gz"), axis=0, tiled=True)
    devices_first = lax.axis_size("gx")
    devices_third = lax.axis_size("gy")
    devices_second = lax.axis_size("gz")
    extent_first, extent_second, extent_third = block.shape
    gathered = gathered.reshape(
        devices_first, devices_third, devices_second, extent_first, extent_second, extent_third
    )
    gathered = jnp.transpose(gathered, (0, 3, 2, 4, 1, 5))
    return gathered.reshape(
        devices_first * extent_first, devices_second * extent_second, devices_third * extent_third
    )


def own_block(whole, width, block_shape):
    padded = jnp.pad(whole, width, mode="wrap")
    starts = (
        lax.axis_index("gx") * block_shape[0],
        lax.axis_index("gz") * block_shape[1],
        lax.axis_index("gy") * block_shape[2],
    )
    extents = (block_shape[0] + 2 * width, block_shape[1] + 2 * width, block_shape[2] + 2 * width)
    return lax.dynamic_slice(padded, starts, extents)


def faces(iterate):
    return extended(iterate, (("gx", 0), ("gy", 2), ("gz", 1)), 1)


def smooth_each(iterate, forcing, weight_nb, diagonal, zero_start):
    if zero_start:
        iterate = DAMPING * forcing / diagonal
    else:
        iterate = relaxed(faces(iterate), forcing, weight_nb, diagonal)
    return iterate


def vcycle_split(grid_level, iterate, forcing, shift_value, zero_start, gather_level):
    weight_nb = 0.25**grid_level
    diagonal = 6.0 * weight_nb + shift_value
    iterate = smooth_each(iterate, forcing, weight_nb, diagonal, zero_start)
    residue = defect(faces(iterate), forcing, weight_nb, diagonal)
    coarse_residue = coarsen(residue)
    if grid_level + 1 < gather_level:
        correction = vcycle_split(
            grid_level + 1, None, coarse_residue, shift_value, True, gather_level
        )
        rim = extended(correction, (("gx", 0), ("gy", 2), ("gz", 1)), 1)
    else:
        whole_residue = collect(coarse_residue)
        whole_correction = vcycle_whole(
            gather_level, jnp.zeros_like(whole_residue), whole_residue, shift_value
        )
        rim = own_block(whole_correction, 1, coarse_residue.shape)
    iterate = iterate + refine(rim, LINEAR_EVEN, LINEAR_ODD)
    iterate = smooth_each(iterate, forcing, weight_nb, diagonal, False)
    return iterate


def per_device(source, shift):
    shift_value = shift[0]
    gather_level = LEVELS - 2
    sources = [source]
    for grid_level in range(1, gather_level + 1):
        sources.append(coarsen(sources[-1]))
    whole_sources = [collect(sources[gather_level])]
    whole_sources.append(coarsen(whole_sources[-1]))
    whole = coarse_solve(whole_sources[-1], shift_value, 0.25 ** (LEVELS - 1))
    grid_level = 2
    whole = refine(wrapped(whole, 2), CUBIC_EVEN, CUBIC_ODD)
    whole = vcycle_whole(grid_level, whole, whole_sources[grid_level - gather_level], shift_value)
    iterate = None
    for grid_level in range(gather_level - 1, -1, -1):
        if grid_level == gather_level - 1:
            rim = own_block(whole, 2, sources[grid_level + 1].shape)
        else:
            rim = extended(iterate, (("gx", 0), ("gy", 2), ("gz", 1)), 2)
        iterate = refine(rim, CUBIC_EVEN, CUBIC_ODD)
        iterate = vcycle_split(
            grid_level, iterate, sources[grid_level], shift_value, False, gather_level
        )
    return iterate


def solution(mesh):
    in_specs = (P("gx", "gz", "gy"), P())
    out_specs = P("gx", "gz", "gy")
    return jax.shard_map(
        per_device, mesh=mesh, in_specs=in_specs, out_specs=out_specs, check_vma=False
    )
```

profile of v0, /device:TPU:0, one launch (start us, length us, event | category | flops | bytes accessed | tf_op | source)
XLA Modules:
  0.0 399.5 jit_solution(12631422108855175203)
XLA Ops:
  2.7 71.1 %all-gather = f32[128,4,32]{2,1,0:T(4,128)S(1)} all-gather(f32[4,4,32]{2,1,0:T(4,128)S(1)} %add_multiply_fusion.7), channel_id=2, replica_groups=mesh['gx'=4,'gy'=4,'gz'=2] {'gx','gy','gz'}, dimensions={0}, use_global_device_ids=true | all-gather | bytes 67584 | tf_op jit(solution)/shard_map/all_gather | solution.py:154
  90.3 2.1 collective-permute-start.1
  92.6 1.4 collective-permute-done
  94.1 1.9 collective-permute-done.1
  98.0 1.7 collective-permute-done.2
  99.9 2.0 collective-permute-start.5
  101.9 1.6 collective-permute-done.4
  104.0 3.6 collective-permute-start.6
  107.6 1.6 collective-permute-done.7
  109.8 1.3 collective-permute-done.9
  111.2 1.6 collective-permute-done.8
  112.9 2.0 collective-permute-start.10
  115.1 1.5 collective-permute-done.10
  116.6 1.9 collective-permute-done.11
  119.1 67.2 %all-gather.1 = f32[128,4,32]{2,1,0:T(4,128)S(1)} all-gather(f32[4,4,32]{2,1,0:T(4,128)S(1)} %add_multiply_fusion.6), channel_id=3, replica_groups=mesh['gx'=4,'gy'=4,'gz'=2] {'gx','gy','gz'}, dimensions={0}, use_global_device_ids=true | all-gather | bytes 67584 | tf_op jit(solution)/shard_map/all_gather | solution.py:154
  194.9 3.8 collective-permute-start.12
  198.7 1.6 collective-permute-done.13
  202.2 1.7 collective-permute-done.14
  204.1 2.0 collective-permute-start.17
  206.1 1.6 collective-permute-done.16
  208.0 3.9 collective-permute-start.19
  211.9 1.6 collective-permute-done.18
  213.5 1.7 collective-permute-start.21
  215.3 1.8 collective-permute-done.20
  217.2 2.0 collective-permute-start.22
  219.3 1.8 collective-permute-done.22
  221.0 1.9 collective-permute-done.23
  223.7 3.9 collective-permute-start.24
  229.6 4.1 %collective-permute-done.25 = f32[1,16,128]{1,2,0:T(8,128)S(1)} collective-permute-done((f32[1,16,128]{1,2,0:T(8,128)S(1)}, f32[1,16,128]{1,2,0:T(8,128)S(1)}, u32[]{:S(2)}, u32[]{:S(2)}) %collective-permute-start.25) | collective-permute-done | bytes 8224 | tf_op jit(solution)/shard_map/ppermute | solution.py:25
  234.4 3.6 collective-permute-done.27
  239.6 1.9 collective-permute-start.29
  241.5 1.7 collective-permute-done.28
  243.8 3.8 collective-permute-start.30
  247.6 1.6 collective-permute-done.31
  249.9 2.8 collective-permute-done.33
  252.7 2.8 collective-permute-done.32
  255.7 1.9 collective-permute-start.34
  257.8 1.7 collective-permute-done.34
  259.5 1.8 collective-permute-done.35
  263.0 3.9 collective-permute-start.36
  266.9 1.5 collective-permute-done.37
  269.0 1.4 collective-permute-done.39
  270.4 1.6 collective-permute-done.38
  272.4 1.8 collective-permute-start.41
  274.2 1.6 collective-permute-done.40
  276.5 68.6 %all-gather.2 = f32[128,4,32]{2,1,0:T(4,128)S(1)} all-gather(f32[4,4,32]{2,1,0:T(4,128)S(1)} %add_multiply_fusion.5), channel_id=4, replica_groups=mesh['gx'=4,'gy'=4,'gz'=2] {'gx','gy','gz'}, dimensions={0}, use_global_device_ids=true | all-gather | bytes 67584 | tf_op jit(solution)/shard_map/all_gather | solution.py:154
  353.7 3.8 collective-permute-start.42
  357.5 1.6 collective-permute-done.43
  359.7 1.3 collective-permute-done.45
  361.0 1.7 collective-permute-done.44
  362.8 2.0 collective-permute-start.47
  364.9 1.6 collective-permute-done.46
  366.8 3.9 collective-permute-start.49
  370.6 1.5 collective-permute-done.48
  372.3 1.7 collective-permute-start.51
  374.0 1.7 collective-permute-done.50
  375.8 2.0 collective-permute-start.52
  377.9 1.6 collective-permute-done.52
  379.5 1.9 collective-permute-done.53
  384.5 2.8 collective-permute-start.54
  387.3 1.6 collective-permute-done.55
  389.6 3.7 collective-permute-done.57
  394.7 1.9 collective-permute-start.59
  396.6 1.7 collective-permute-done.58
  (445 shorter events, 58.4 us)
Async XLA Ops:
  90.1 4.0 collective-permute-start
  90.3 5.8 %collective-permute-start.1 = (f32[1,8,64]{1,2,0:T(8,128)S(1)}, f32[1,8,64]{1,2,0:T(8,128)S(1)}, u32[]{:S(2)}, u32[]{:S(2)}) collective-permute-start(f32[1,8,64]{1,2,0:T(8,128)S(1)} %bitcast.417), channel_id=1, source_target_pairs={{0,8},{8,16},{16,24},{24,0},{1,9},{9,17},{17,25},{25,1},{2,10},{10... | collective-permute-start | bytes 6152 | tf_op jit(solution)/shard_map/ppermute | solution.py:25
  96.2 1.8 collective-permute-start.3
  96.2 3.5 collective-permute-start.2
  99.8 3.7 collective-permute-start.4
  99.9 3.7 collective-permute-start.5
  103.7 5.5 %collective-permute-start.7 = (f32[1,8,64]{2,1,0:T(8,128)S(1)}, f32[1,8,64]{2,1,0:T(8,128)S(1)}, u32[]{:S(2)}, u32[]{:S(2)}) collective-permute-start(f32[1,8,64]{2,1,0:T(8,128)S(1)} %get-tuple-element.179), channel_id=1, source_target_pairs={{0,8},{8,16},{16,24},{24,0},{1,9},{9,17},{17,25},{25,1},{2,10},{10... | collective-permute-start | bytes 6152 | tf_op jit(solution)/shard_map/ppermute | solution.py:25
  104.0 5.2 %collective-permute-start.6 = (f32[1,8,64]{2,1,0:T(8,128)S(1)}, f32[1,8,64]{2,1,0:T(8,128)S(1)}, u32[]{:S(2)}, u32[]{:S(2)}) collective-permute-start(f32[1,8,64]{2,1,0:T(8,128)S(1)} %get-tuple-element.180), channel_id=1, source_target_pairs={{8,0},{16,8},{24,16},{0,24},{9,1},{17,9},{25,17},{1,25},{10,2},{18... | collective-permute-start | bytes 6152 | tf_op jit(solution)/shard_map/ppermute | solution.py:28
  109.3 1.9 collective-permute-start.9
  109.3 3.5 collective-permute-start.8
  112.9 3.7 collective-permute-start.10
  114.9 3.6 collective-permute-start.11
  194.8 5.5 %collective-permute-start.13 = (f32[1,8,64]{2,1,0:T(8,128)S(1)}, f32[1,8,64]{2,1,0:T(8,128)S(1)}, u32[]{:S(2)}, u32[]{:S(2)}) collective-permute-start(f32[1,8,64]{2,1,0:T(8,128)S(1)} %get-tuple-element.175), channel_id=1, source_target_pairs={{0,8},{8,16},{16,24},{24,0},{1,9},{9,17},{17,25},{25,1},{2,10},{10... | collective-permute-start | bytes 6152 | tf_op jit(solution)/shard_map/ppermute | solution.py:25
  194.9 5.4 %collective-permute-start.12 = (f32[1,8,64]{2,1,0:T(8,128)S(1)}, f32[1,8,64]{2,1,0:T(8,128)S(1)}, u32[]{:S(2)}, u32[]{:S(2)}) collective-permute-start(f32[1,8,64]{2,1,0:T(8,128)S(1)} %get-tuple-element.176), channel_id=1, source_target_pairs={{8,0},{16,8},{24,16},{0,24},{9,1},{17,9},{25,17},{1,25},{10,2},{18... | collective-permute-start | bytes 6152 | tf_op jit(solution)/shard_map/ppermute | solution.py:28
  200.4 1.8 collective-permute-start.15
  200.4 3.5 collective-permute-start.14
  204.0 3.7 collective-permute-start.16
  204.1 3.7 collective-permute-start.17
  207.9 5.5 %collective-permute-start.18 = (f32[2,8,64]{2,1,0:T(8,128)S(1)}, f32[2,8,64]{2,1,0:T(8,128)S(1)}, u32[]{:S(2)}, u32[]{:S(2)}) collective-permute-start(f32[2,8,64]{2,1,0:T(8,128)S(1)} %get-tuple-element.173), channel_id=1, source_target_pairs={{0,8},{8,16},{16,24},{24,0},{1,9},{9,17},{17,25},{25,1},{2,10},{10... | collective-permute-start | bytes 12296 | tf_op jit(solution)/shard_map/ppermute | solution.py:25
  208.0 5.4 %collective-permute-start.19 = (f32[2,8,64]{2,1,0:T(8,128)S(1)}, f32[2,8,64]{2,1,0:T(8,128)S(1)}, u32[]{:S(2)}, u32[]{:S(2)}) collective-permute-start(f32[2,8,64]{2,1,0:T(8,128)S(1)} %get-tuple-element.174), channel_id=1, source_target_pairs={{8,0},{16,8},{24,16},{0,24},{9,1},{17,9},{25,17},{1,25},{10,2},{18... | collective-permute-start | bytes 12296 | tf_op jit(solution)/shard_map/ppermute | solution.py:28
  213.5 3.5 collective-permute-start.20
  213.5 3.5 collective-permute-start.21
  217.2 3.8 collective-permute-start.22
  219.2 3.7 collective-permute-start.23
  223.7 5.8 %collective-permute-start.24 = (f32[1,16,128]{1,2,0:T(8,128)S(1)}, f32[1,16,128]{1,2,0:T(8,128)S(1)}, u32[]{:S(2)}, u32[]{:S(2)}) collective-permute-start(f32[1,16,128]{1,2,0:T(8,128)S(1)} %bitcast.415), channel_id=1, source_target_pairs={{8,0},{16,8},{24,16},{0,24},{9,1},{17,9},{25,17},{1,25},{10,2},{18... | collective-permute-start | bytes 24584 | tf_op jit(solution)/shard_map/ppermute | solution.py:28
  227.6 6.1 %collective-permute-start.25 = (f32[1,16,128]{1,2,0:T(8,128)S(1)}, f32[1,16,128]{1,2,0:T(8,128)S(1)}, u32[]{:S(2)}, u32[]{:S(2)}) collective-permute-start(f32[1,16,128]{1,2,0:T(8,128)S(1)} %bitcast.414), channel_id=1, source_target_pairs={{0,8},{8,16},{16,24},{24,0},{1,9},{9,17},{17,25},{25,1},{2,10},{10... | collective-permute-start | bytes 24584 | tf_op jit(solution)/shard_map/ppermute | solution.py:25
  233.9 4.2 %collective-permute-start.27 = (f32[18,16,1]{2,1,0:T(8,128)S(1)}, f32[18,16,1]{2,1,0:T(8,128)S(1)}, u32[]{:S(2)}, u32[]{:S(2)}) collective-permute-start(f32[18,16,1]{2,1,0:T(8,128)S(1)} %get-tuple-element.19), channel_id=1, source_target_pairs={{2,0},{4,2},{6,4},{0,6},{3,1},{5,3},{7,5},{1,7},{10,8},{12,10},{14... | collective-permute-start | bytes 3464 | tf_op jit(solution)/shard_map/ppermute | solution.py:28
  233.9 9.5 %copy-start = (f32[16,16,128]{2,1,0:T(8,128)S(1)}, f32[16,16,128]{2,1,0:T(8,128)}, u32[]{:S(2)}) copy-start(f32[16,16,128]{2,1,0:T(8,128)} %param.2) | copy-start | bytes 393220
  233.9 5.3 %collective-permute-start.26 = (f32[18,16,1]{2,1,0:T(8,128)S(1)}, f32[18,16,1]{2,1,0:T(8,128)S(1)}, u32[]{:S(2)}, u32[]{:S(2)}) collective-permute-start(f32[18,16,1]{2,1,0:T(8,128)S(1)} %get-tuple-element.20), channel_id=1, source_target_pairs={{0,2},{2,4},{4,6},{6,0},{1,3},{3,5},{5,7},{7,1},{8,10},{10,12},{12... | collective-permute-start | bytes 3464 | tf_op jit(solution)/shard_map/ppermute | solution.py:25
  239.4 3.8 collective-permute-start.28
  239.6 3.8 collective-permute-start.29
  243.7 5.5 %collective-permute-start.31 = (f32[1,16,128]{2,1,0:T(8,128)S(1)}, f32[1,16,128]{2,1,0:T(8,128)S(1)}, u32[]{:S(2)}, u32[]{:S(2)}) collective-permute-start(f32[1,16,128]{2,1,0:T(8,128)S(1)} %get-tuple-element.29), channel_id=1, source_target_pairs={{0,8},{8,16},{16,24},{24,0},{1,9},{9,17},{17,25},{25,1},{2,10},{10... | collective-permute-start | bytes 24584 | tf_op jit(solution)/shard_map/ppermute | solution.py:25
  243.8 5.4 %collective-permute-start.30 = (f32[1,16,128]{2,1,0:T(8,128)S(1)}, f32[1,16,128]{2,1,0:T(8,128)S(1)}, u32[]{:S(2)}, u32[]{:S(2)}) collective-permute-start(f32[1,16,128]{2,1,0:T(8,128)S(1)} %get-tuple-element.30), channel_id=1, source_target_pairs={{8,0},{16,8},{24,16},{0,24},{9,1},{17,9},{25,17},{1,25},{10,2},{18... | collective-permute-start | bytes 24584 | tf_op jit(solution)/shard_map/ppermute | solution.py:28
  249.3 3.4 collective-permute-start.33
  249.4 6.1 %collective-permute-start.32 = (f32[18,16,1]{2,1,0:T(8,128)S(1)}, f32[18,16,1]{2,1,0:T(8,128)S(1)}, u32[]{:S(2)}, u32[]{:S(2)}) collective-permute-start(f32[18,16,1]{2,1,0:T(8,128)S(1)} %get-tuple-element.18), channel_id=1, source_target_pairs={{0,2},{2,4},{4,6},{6,0},{1,3},{3,5},{5,7},{7,1},{8,10},{10,12},{12... | collective-permute-start | bytes 3464 | tf_op jit(solution)/shard_map/ppermute | solution.py:25
  255.7 3.8 collective-permute-start.34
  257.6 3.8 collective-permute-start.35
  263.0 5.5 %collective-permute-start.37 = (f32[1,8,64]{2,1,0:T(8,128)S(1)}, f32[1,8,64]{2,1,0:T(8,128)S(1)}, u32[]{:S(2)}, u32[]{:S(2)}) collective-permute-start(f32[1,8,64]{2,1,0:T(8,128)S(1)} %get-tuple-element.171), channel_id=1, source_target_pairs={{0,8},{8,16},{16,24},{24,0},{1,9},{9,17},{17,25},{25,1},{2,10},{10... | collective-permute-start | bytes 6152 | tf_op jit(solution)/shard_map/ppermute | solution.py:25
  263.0 5.4 %collective-permute-start.36 = (f32[1,8,64]{2,1,0:T(8,128)S(1)}, f32[1,8,64]{2,1,0:T(8,128)S(1)}, u32[]{:S(2)}, u32[]{:S(2)}) collective-permute-start(f32[1,8,64]{2,1,0:T(8,128)S(1)} %get-tuple-element.172), channel_id=1, source_target_pairs={{8,0},{16,8},{24,16},{0,24},{9,1},{17,9},{25,17},{1,25},{10,2},{18... | collective-permute-start | bytes 6152 | tf_op jit(solution)/shard_map/ppermute | solution.py:28
  268.5 1.9 collective-permute-start.39
  268.5 3.5 collective-permute-start.38
  272.1 3.7 collective-permute-start.40
  272.4 3.6 collective-permute-start.41
  353.6 5.5 %collective-permute-start.43 = (f32[1,8,64]{2,1,0:T(8,128)S(1)}, f32[1,8,64]{2,1,0:T(8,128)S(1)}, u32[]{:S(2)}, u32[]{:S(2)}) collective-permute-start(f32[1,8,64]{2,1,0:T(8,128)S(1)} %get-tuple-element.167), channel_id=1, source_target_pairs={{0,8},{8,16},{16,24},{24,0},{1,9},{9,17},{17,25},{25,1},{2,10},{10... | collective-permute-start | bytes 6152 | tf_op jit(solution)/shard_map/ppermute | solution.py:25
  353.7 5.4 %collective-permute-start.42 = (f32[1,8,64]{2,1,0:T(8,128)S(1)}, f32[1,8,64]{2,1,0:T(8,128)S(1)}, u32[]{:S(2)}, u32[]{:S(2)}) collective-permute-start(f32[1,8,64]{2,1,0:T(8,128)S(1)} %get-tuple-element.168), channel_id=1, source_target_pairs={{8,0},{16,8},{24,16},{0,24},{9,1},{17,9},{25,17},{1,25},{10,2},{18... | collective-permute-start | bytes 6152 | tf_op jit(solution)/shard_map/ppermute | solution.py:28
  359.2 1.8 collective-permute-start.45
  359.2 3.5 collective-permute-start.44
  362.8 3.7 collective-permute-start.46
  362.8 3.7 collective-permute-start.47
  366.7 5.5 %collective-permute-start.48 = (f32[1,8,64]{2,1,0:T(8,128)S(1)}, f32[1,8,64]{2,1,0:T(8,128)S(1)}, u32[]{:S(2)}, u32[]{:S(2)}) collective-permute-start(f32[1,8,64]{2,1,0:T(8,128)S(1)} %get-tuple-element.165), channel_id=1, source_target_pairs={{0,8},{8,16},{16,24},{24,0},{1,9},{9,17},{17,25},{25,1},{2,10},{10... | collective-permute-start | bytes 6152 | tf_op jit(solution)/shard_map/ppermute | solution.py:25
  366.8 5.4 %collective-permute-start.49 = (f32[1,8,64]{2,1,0:T(8,128)S(1)}, f32[1,8,64]{2,1,0:T(8,128)S(1)}, u32[]{:S(2)}, u32[]{:S(2)}) collective-permute-start(f32[1,8,64]{2,1,0:T(8,128)S(1)} %get-tuple-element.166), channel_id=1, source_target_pairs={{8,0},{16,8},{24,16},{0,24},{9,1},{17,9},{25,17},{1,25},{10,2},{18... | collective-permute-start | bytes 6152 | tf_op jit(solution)/shard_map/ppermute | solution.py:28
  372.3 3.4 collective-permute-start.50
  372.3 3.4 collective-permute-start.51
  375.8 3.7 collective-permute-start.52
  377.8 3.6 collective-permute-start.53
  383.3 5.6 %collective-permute-start.55 = (f32[1,16,128]{2,1,0:T(8,128)S(1)}, f32[1,16,128]{2,1,0:T(8,128)S(1)}, u32[]{:S(2)}, u32[]{:S(2)}) collective-permute-start(f32[1,16,128]{2,1,0:T(8,128)S(1)} %get-tuple-element.25), channel_id=1, source_target_pairs={{0,8},{8,16},{16,24},{24,0},{1,9},{9,17},{17,25},{25,1},{2,10},{10... | collective-permute-start | bytes 24584 | tf_op jit(solution)/shard_map/ppermute | solution.py:25
  384.5 4.4 %collective-permute-start.54 = (f32[1,16,128]{2,1,0:T(8,128)S(1)}, f32[1,16,128]{2,1,0:T(8,128)S(1)}, u32[]{:S(2)}, u32[]{:S(2)}) collective-permute-start(f32[1,16,128]{2,1,0:T(8,128)S(1)} %get-tuple-element.26), channel_id=1, source_target_pairs={{8,0},{16,8},{24,16},{0,24},{9,1},{17,9},{25,17},{1,25},{10,2},{18... | collective-permute-start | bytes 24584 | tf_op jit(solution)/shard_map/ppermute | solution.py:28
  389.0 4.2 %collective-permute-start.57 = (f32[18,16,1]{2,1,0:T(8,128)S(1)}, f32[18,16,1]{2,1,0:T(8,128)S(1)}, u32[]{:S(2)}, u32[]{:S(2)}) collective-permute-start(f32[18,16,1]{2,1,0:T(8,128)S(1)} %get-tuple-element.15), channel_id=1, source_target_pairs={{2,0},{4,2},{6,4},{0,6},{3,1},{5,3},{7,5},{1,7},{10,8},{12,10},{14... | collective-permute-start | bytes 3464 | tf_op jit(solution)/shard_map/ppermute | solution.py:28
  389.1 5.3 %collective-permute-start.56 = (f32[18,16,1]{2,1,0:T(8,128)S(1)}, f32[18,16,1]{2,1,0:T(8,128)S(1)}, u32[]{:S(2)}, u32[]{:S(2)}) collective-permute-start(f32[18,16,1]{2,1,0:T(8,128)S(1)} %get-tuple-element.16), channel_id=1, source_target_pairs={{0,2},{2,4},{4,6},{6,0},{1,3},{3,5},{5,7},{7,1},{8,10},{10,12},{12... | collective-permute-start | bytes 3464 | tf_op jit(solution)/shard_map/ppermute | solution.py:25
  394.5 3.8 collective-permute-start.58
  394.7 3.8 collective-permute-start.59
where the time goes:
time: 400 us; the launch traced here: 399 us
  blocking collectives  207 us (52%)
  waiting for transfers between devices  78.8 us (20%)
  starting transfers between devices  65.9 us (16%)
  matrix products  18.9 us (5%)
  local copies, waits for them, and re-layouts  16.2 us (4%)
  other arithmetic  9.75 us (2%)
    all_gather x3, blocking collectives, collect(): lax.all_gather(block[None], ('gx', 'gy', 'gz'), axis=0, tiled=True)  207 us
    ppermute x30, waiting for transfers between devices, extended(): lax.ppermute(lax.slice_in_dim(block, block.shape[dim] - width, None, axis...  43.3 us
    ppermute x30, starting transfers between devices, extended(): lax.ppermute(lax.slice_in_dim(block, 0, width, axis=dim), axis, backward)  42.1 us
    ppermute x30, waiting for transfers between devices, extended(): lax.ppermute(lax.slice_in_dim(block, 0, width, axis=dim), axis, backward)  35.5 us
    ppermute x30, starting transfers between devices, extended(): lax.ppermute(lax.slice_in_dim(block, block.shape[dim] - width, None, axis...  23.8 us
    dot_general x80, matrix products, along_axis(): jnp.tensordot(matrix, values, axes=([1], [dimension]), precision=PRECISE)  18.9 us
  transfers between devices with their start and end apart: 60, of which 50 were waited for; matrix products, arithmetic and copies ran while one was open for 0% of the time, Pallas kernels for 0%

commit v1 on v0

v1 whole, which is shorter than its diff:
```python
import functools

import jax
import jax.numpy as jnp
import numpy as np
from jax import lax
from jax.experimental import pallas as pl
from jax.experimental.pallas import tpu as pltpu
from jax.sharding import PartitionSpec as P

LEVELS = 4
DAMPING = 6.0 / 7.0
PRECISE = lax.Precision.HIGHEST
CUBIC = (
    {-2: -5.0 / 128.0, -1: 35.0 / 128.0, 0: 105.0 / 128.0, 1: -7.0 / 128.0},
    {-1: -7.0 / 128.0, 0: 105.0 / 128.0, 1: 35.0 / 128.0, 2: -5.0 / 128.0},
)
LINEAR = ({-1: 0.25, 0: 0.75}, {0: 0.75, 1: 0.25})
NAMES = ("gx", "gy", "gz")


def basis(count):
    cells = np.arange(count)
    columns, cosines = [], []
    for m in range(count):
        k = (m + 1) // 2
        angle = 2.0 * np.pi * k * cells / count
        column = np.cos(angle) if m % 2 == 1 or m == 0 else np.sin(angle)
        columns.append(column / np.sqrt(np.sum(column**2)))
        cosines.append(np.cos(2.0 * np.pi * k / count))
    return np.stack(columns, axis=1), np.array(cosines, np.float32)


def interpolation(coarse_count, fine_cells, weights):
    matrix = np.zeros((len(fine_cells), coarse_count))
    for row, cell in enumerate(fine_cells):
        for offset, weight in weights[cell % 2].items():
            matrix[row, (cell // 2 + offset) % coarse_count] += weight
    return matrix


def pairs(coarse_count):
    return np.kron(np.eye(coarse_count), np.ones((1, 2)))


def blocked(matrix):
    count = max(1, 128 // matrix.shape[1])
    return np.kron(np.eye(count), matrix)


def constants(block, sizes):
    b0, b1, b2 = block
    m0, m1, m2 = (size // 2 for size in sizes)
    q0, q1, q2 = (size // 4 for size in sizes)
    c0, c1, c2 = (size // 8 for size in sizes)
    table = {}
    table["own_rows"] = np.kron(np.eye(b0 // 2), pairs(b1 // 2))
    lanes = 0.125 * pairs(b2 // 2).T
    table["own_lo"] = np.concatenate([lanes, np.zeros_like(lanes)], axis=1)
    table["own_hi"] = np.concatenate([np.zeros_like(lanes), lanes], axis=1)
    table["down_rows"] = blocked(pairs(q1))
    table["down_lanes"] = 0.125 * pairs(q2).T
    window_lanes = [b2 + j for j in range(b2 // 2)] + [j - b2 for j in range(b2 // 2, 2 * b2)]
    window_rows = [j - 8 for j in range(b1 + 16)]
    for name, weights in (("cubic", CUBIC), ("linear", LINEAR)):
        table[name + "_rows1"] = blocked(interpolation(q1, range(m1), weights))
        table[name + "_lanes1"] = interpolation(q2, range(m2), weights).T
        table[name + "_rows0"] = blocked(interpolation(m1, window_rows, weights))
        table[name + "_lanes0"] = interpolation(m2, window_lanes, weights).T
    (u0, cos0), (u1, cos1), (u2, cos2) = basis(c0), basis(c1), basis(c2)
    table["spectrum_rows"] = np.kron(u0.T @ pairs(c0), u1.T @ pairs(c1))
    table["spectrum_lanes"] = 0.125 * pairs(c2).T @ u2
    for name, weights in (("cubic", CUBIC), ("linear", LINEAR)):
        table[name + "_rows2"] = np.kron(
            interpolation(c0, range(q0), weights) @ u0, interpolation(c1, range(q1), weights) @ u1
        )
        table[name + "_lanes2"] = u2.T @ interpolation(c2, range(q2), weights).T
    two = np.float32(2.0)
    eigen = (
        np.float32(6.0)
        - two * cos0[:, None, None]
        - two * cos1[None, :, None]
        - two * cos2[None, None, :]
    )
    table["eigen"] = (np.float32(0.25 ** (LEVELS - 1)) * eigen).reshape(c0 * c1, c2)
    return {name: np.asarray(value, np.float32) for name, value in table.items()}


def dot(a, b):
    return jnp.dot(a, b, precision=PRECISE, preferred_element_type=jnp.float32)


def around(plane):
    rows, lanes = plane.shape
    total = pltpu.roll(plane, 1, 0) + pltpu.roll(plane, rows - 1, 0)
    return total + (pltpu.roll(plane, 1, 1) + pltpu.roll(plane, lanes - 1, 1))


def around_all(values):
    first = jnp.concatenate([values[1:], values[:1]], axis=0)
    first = first + jnp.concatenate([values[-1:], values[:-1]], axis=0)
    for axis in (1, 2):
        first = first + pltpu.roll(values, 1, axis)
        first = first + pltpu.roll(values, values.shape[axis] - 1, axis)
    return first


def row_blocks(matrix, values):
    depth = matrix.shape[1]
    return jnp.concatenate(
        [dot(matrix, values[i : i + depth]) for i in range(0, values.shape[0], depth)], axis=0
    )


def loop(count, body):
    def step(i, carry):
        body(i)
        return carry

    lax.fori_loop(0, count, step, 0, unroll=4 if count % 4 == 0 else 2)


def close(ref):
    count = ref.shape[0] - 2
    ref[0] = ref[count]
    ref[count + 1] = ref[1]


def defect_plane(v, p, g, weight, diagonal):
    center = v[p]
    beside = v[p - 1] + v[p + 1] + around(center)
    return center, g - (diagonal * center - weight * beside)


def restrict_own(k, summed):
    b_half, rows, lanes = summed.shape
    folded = dot(k["own_rows"][...], summed.reshape(b_half * rows, lanes))
    half = folded.shape[0] // 2
    return dot(folded[:half], k["own_lo"][...]) + dot(folded[half:], k["own_hi"][...])


def unpack(gathered, counts, g):
    nx, ny, nz = counts
    x, y, z = (lax.axis_index(name) for name in NAMES)
    half, rows, lanes = gathered.shape[1:]
    low = lax.broadcasted_iota(jnp.int32, (half, rows, lanes), 2) < lanes // 2
    for dx in range(nx):
        for dz in range(nz):
            for pair in range(ny // 2):
                parts = []
                for dy in (2 * pair, 2 * pair + 1):
                    index = (lax.rem(x + dx, nx) * ny + lax.rem(y + dy, ny)) * nz
                    parts.append(gathered[index + lax.rem(z + dz, nz)])
                turned = [pltpu.roll(part, lanes // 2, 2) for part in parts]
                where = (pl.ds(dz * rows, rows), pl.ds(pair * lanes, lanes))
                start = 2 * half * dx
                g[(pl.ds(start, half), *where)] = jnp.where(low, parts[0], turned[1])
                g[(pl.ds(start + half, half), *where)] = jnp.where(low, turned[0], parts[1])


def solve(k, kind, values, shift):
    shape = values.shape
    flat = values.reshape(shape[0] * shape[1], shape[2])
    spectrum = dot(k["spectrum_rows"][...], dot(flat, k["spectrum_lanes"][...]))
    spectrum = spectrum / (k["eigen"][...] + shift)
    fine = dot(k[kind + "_rows2"][...], dot(spectrum, k[kind + "_lanes2"][...]))
    return fine.reshape(shape)


def cycle2(k, v, g, shift):
    weight = 0.25**2
    diagonal = 6.0 * weight + shift
    damp = DAMPING / diagonal
    if v is None:
        v = damp * g
    else:
        v = v + damp * (g - (diagonal * v - weight * around_all(v)))
    v = v + solve(k, "linear", g - (diagonal * v - weight * around_all(v)), shift)
    return v + damp * (g - (diagonal * v - weight * around_all(v)))


def down(k, t, shape2):
    flat = row_blocks(k["down_rows"][...], t[...].reshape(-1, t.shape[2]))
    return dot(flat, k["down_lanes"][...]).reshape(shape2)


def up(k, kind, level, values, z):
    flat = dot(values, k[kind + "_lanes" + level][...])
    z[...] = row_blocks(k[kind + "_rows" + level][...], flat).reshape(z.shape)


def blend(z, i, weights, count):
    total = None
    for offset, weight in weights.items():
        index = i + offset
        index = index if count is None else lax.rem(index + count, count)
        term = weight * z[index]
        total = term if total is None else total + term
    return total


def up1(k, kind, values, z, v, add):
    count = z.shape[0]
    up(k, kind, "1", values.reshape(-1, values.shape[2]), z)
    weights = CUBIC if kind == "cubic" else LINEAR

    def body(i):
        for odd in (0, 1):
            p = 2 * i + odd + 1
            value = blend(z, i, weights[odd], count)
            v[p] = v[p] + value if add else value

    loop(count, body)
    close(v)


def cycle1(k, v, u, g, t, z, shift, zero, shape2):
    weight = 0.25
    diagonal = 6.0 * weight + shift
    damp = DAMPING / diagonal
    count = g.shape[0]

    def before(p):
        if zero:
            u[p + 1] = damp * g[p]
        else:
            center, rest = defect_plane(v, p + 1, g[p], weight, diagonal)
            u[p + 1] = center + damp * rest

    loop(count, before)
    close(u)

    def residue(i):
        t[i] = (
            defect_plane(u, 2 * i + 1, g[2 * i], weight, diagonal)[1]
            + defect_plane(u, 2 * i + 2, g[2 * i + 1], weight, diagonal)[1]
        )

    loop(count // 2, residue)
    correction = cycle2(k, None, down(k, t, shape2), shift)
    up1(k, "linear", correction, z, u, True)

    def after(p):
        center, rest = defect_plane(u, p + 1, g[p], weight, diagonal)
        v[p + 1] = center + damp * rest

    loop(count, after)
    close(v)


def window(k, kind, v, zw, span, write):
    count = v.shape[0] - 2
    values = jnp.concatenate([v[count - 3 : count + 1], v[1 : span - 3]], axis=0)
    up(k, kind, "0", values.reshape(-1, values.shape[2]), zw)
    weights = CUBIC if kind == "cubic" else LINEAR

    def body(i):
        for odd in (0, 1):
            write(2 * i + odd, blend(zw, i + 3, weights[odd], None))

    loop(span - 6, body)


def own_defect(v, p, f, weight, diagonal):
    rows, lanes = f.shape
    inside = (pl.ds(8, rows), pl.ds(lanes, lanes))
    wide = v[p + 1, pl.ds(8, rows), :]
    center = wide[:, lanes:]
    beside = v[(p, *inside)] + v[(p + 2, *inside)]
    beside = beside + v[p + 1, pl.ds(7, rows), pl.ds(lanes, lanes)]
    beside = beside + v[p + 1, pl.ds(9, rows), pl.ds(lanes, lanes)]
    beside = beside + pltpu.roll(wide, 1, 1)[:, lanes:]
    beside = beside + pltpu.roll(wide, 2 * lanes - 1, 1)[:, lanes:]
    return center, f - (diagonal * center - weight * beside)


def first_kernel(names, *refs):
    k = dict(zip(names, refs))
    source, out = refs[len(names) :]
    b0, b1, b2 = source.shape
    summed = source[...].reshape(b0 // 2, 2, b1, b2)
    out[...] = restrict_own(k, summed[:, 0] + summed[:, 1]).reshape(out.shape)


def second_kernel(names, counts, shape2, span, *refs):
    k = dict(zip(names, refs))
    (shift_ref, gathered, source, plane_lo, plane_hi, row_lo, row_hi, lane_halo) = refs[
        len(names) : len(names) + 8
    ]
    out, v1, g, v, u, t, z, zw, v0, f, summed = refs[len(names) + 8 :]
    shift = shift_ref[0]
    unpack(gathered, counts, g)
    b0, b1, b2 = source.shape
    f[...] = jnp.zeros_like(f)
    rows, lanes = pl.ds(8, b1), pl.ds(b2, b2)
    f[1 : b0 + 1, rows, lanes] = source[...]
    f[0, rows, lanes] = plane_lo[0]
    f[b0 + 1, rows, lanes] = plane_hi[0]
    f[1 : b0 + 1, pl.ds(7, 1), lanes] = row_lo[...]
    f[1 : b0 + 1, pl.ds(8 + b1, 1), lanes] = row_hi[...]
    f[1 : b0 + 1, rows, pl.ds(0, b2)] = lane_halo[...]
    def pair_sum(i):
        t[i] = g[2 * i] + g[2 * i + 1]

    loop(g.shape[0] // 2, pair_sum)
    forcing2 = down(k, t, shape2)
    iterate2 = cycle2(k, solve(k, "cubic", forcing2, shift), forcing2, shift)
    up1(k, "cubic", iterate2, z, v, False)
    cycle1(k, v, u, g, t, z, shift, False, shape2)

    def put(p, value):
        v0[p] = value

    window(k, "cubic", v, zw, span, put)
    diagonal = 6.0 + shift
    damp = DAMPING / diagonal

    def before(p):
        center, rest = defect_plane(v0, p + 1, f[p], 1.0, diagonal)
        v1[p] = center + damp * rest

    loop(b0 + 2, before)

    def residue(i):
        summed[i] = (
            own_defect(v1, 2 * i, source[2 * i], 1.0, diagonal)[1]
            + own_defect(v1, 2 * i + 1, source[2 * i + 1], 1.0, diagonal)[1]
        )

    loop(b0 // 2, residue)
    out[...] = restrict_own(k, summed[...]).reshape(out.shape)


def third_kernel(names, counts, shape2, span, *refs):
    k = dict(zip(names, refs))
    shift_ref, gathered, source, v1, out, g, v, u, t, z, zw, w = refs[len(names) :]
    shift = shift_ref[0]
    unpack(gathered, counts, g)
    cycle1(k, v, u, g, t, z, shift, True, shape2)
    b0 = source.shape[0]

    def put(p, value):
        w[p] = value

    window(k, "linear", v, zw, span, put)

    def add(p):
        w[p] = v1[p] + w[p + 1]

    loop(b0 + 2, add)
    diagonal = 6.0 + shift
    damp = DAMPING / diagonal

    def after(p):
        center, rest = own_defect(w, p, source[p], 1.0, diagonal)
        out[p] = center + damp * rest

    loop(b0, after)


def beside(values, axis, step):
    count = lax.axis_size(axis)
    return lax.ppermute(values, axis, [(i, (i + step) % count) for i in range(count)])


def per_device(counts, source, shift):
    nx, ny, nz = counts
    b0, b1, b2 = source.shape
    sizes = (b0 * nx, b1 * nz, b2 * ny)
    table = constants(source.shape, sizes)
    m0, m1, m2 = (size // 2 for size in sizes)
    shape2 = tuple(size // 4 for size in sizes)
    span = b0 // 2 + 8
    wide = (b1 + 16, 2 * b2)
    packed = jax.ShapeDtypeStruct((b0 // 4, b1 // 2, b2), jnp.float32)
    vmem = pl.BlockSpec(memory_space=pltpu.VMEM)
    params = pltpu.CompilerParams(vmem_limit_bytes=60 * 1024 * 1024)

    def field(*shape):
        return pltpu.VMEM(shape, jnp.float32)

    def run(body, names, operands, outs, scratch, smem):
        specs = [vmem] * len(names)
        specs += [pl.BlockSpec(memory_space=pltpu.SMEM)] * smem
        specs += [vmem] * (len(operands) - smem)
        return pl.pallas_call(
            functools.partial(body, names),
            out_shape=outs,
            in_specs=specs,
            out_specs=[vmem] * len(outs) if isinstance(outs, tuple) else vmem,
            scratch_shapes=scratch,
            compiler_params=params,
        )(*[jnp.asarray(table[name]) for name in names], *operands)

    own = ("own_rows", "own_lo", "own_hi")
    coarse = ("down_rows", "down_lanes", "spectrum_rows", "spectrum_lanes", "eigen")
    linear = tuple(name for name in table if name.startswith("linear"))
    linear_low = tuple(name for name in linear if not name.endswith("0"))
    cubic = tuple(name for name in table if name.startswith("cubic"))
    plane_lo = beside(source[-1:], "gx", 1)
    plane_hi = beside(source[:1], "gx", -1)
    row_lo = beside(source[:, -1:], "gz", 1)
    row_hi = beside(source[:, :1], "gz", -1)
    lane_lo = beside(source[:, :, -1], "gy", 1)
    lane_hi = beside(source[:, :, 0], "gy", -1)
    lane_halo = jnp.concatenate(
        [lane_hi[:, :, None], jnp.zeros((b0, b1, b2 - 2), jnp.float32), lane_lo[:, :, None]], axis=2
    )
    buffers = [
        field(m0, m1, m2),
        field(m0 + 2, m1, m2),
        field(m0 + 2, m1, m2),
        field(m0 // 2, m1, m2),
        field(m0 // 2, m1, m2),
        field(span, *wide),
    ]
    block = run(first_kernel, own, (source,), packed, [], 0)
    gathered = lax.all_gather(block, NAMES, axis=0)
    block, v1 = run(
        lambda names, *refs: second_kernel(names, counts, shape2, span, *refs),
        own + coarse + linear_low + cubic,
        (shift, gathered, source, plane_lo, plane_hi, row_lo, row_hi, lane_halo),
        (packed, jax.ShapeDtypeStruct((b0 + 2, *wide), jnp.float32)),
        buffers + [field(b0 + 4, *wide), field(b0 + 2, *wide), field(b0 // 2, b1, b2)],
        1,
    )
    gathered = lax.all_gather(block, NAMES, axis=0)
    return run(
        lambda names, *refs: third_kernel(names, counts, shape2, span, *refs),
        coarse + linear,
        (shift, gathered, source, v1),
        jax.ShapeDtypeStruct(source.shape, jnp.float32),
        buffers + [field(b0 + 4, *wide)],
        1,
    )


def solution(mesh):
    counts = tuple(mesh.shape[name] for name in NAMES)
    return jax.shard_map(
        functools.partial(per_device, counts),
        mesh=mesh,
        in_specs=(P("gx", "gz", "gy"), P()),
        out_specs=P("gx", "gz", "gy"),
        check_vma=False,
    )
```

time: 400 us -> 188 us (0.47)
  waiting for transfers between devices: 78.8 us -> 4.3 us
  blocking collectives: 207 us -> 145 us
  starting transfers between devices: 65.9 us -> 8.99 us
  Pallas kernels: 0 us -> 24 us
  matrix products: 18.9 us -> 0 us
  local copies, waits for them, and re-layouts: 16.2 us -> 3.98 us
  other arithmetic: 9.75 us -> 0.76 us
    ppermute x60 -> x6, waiting for transfers between devices: 78.8 us -> 4.3 us  [beside(): lax.ppermute(values, axis, [(i, (i + step) % count) for i in range(count)])]
    all_gather x3 -> x2, blocking collectives: 207 us -> 145 us  [per_device(): gathered = lax.all_gather(block, NAMES, axis=0)]
    ppermute x60 -> x6, starting transfers between devices: 65.9 us -> 8.99 us  [beside(): lax.ppermute(values, axis, [(i, (i + step) % count) for i in range(count)])]
    pallas_call x0 -> x3, Pallas kernels: none -> 24 us  [run(): pl.pallas_call(functools.partial(body, names), out_shape=outs, in_specs=s...]
    dot_general x80 -> x0, matrix products: 18.9 us -> none  [along_axis(): jnp.tensordot(matrix, values, axes=([1], [dimension]), precision=PRECISE)]
    slice x92 -> x3, local copies, waits for them, and re-layouts: 9.19 us -> 2.67 us  [the longest x1 1.07 us: per_device(): lane_hi = beside(source[:, :, 0], 'gy', -1)]
  transfers between devices with their start and end apart: 60 -> 6, of which waited for: 50 -> 1; matrix products, arithmetic and copies ran while one was open for 0% -> 2% of each run, Pallas kernels for 0% -> 1%
where the time goes in v1:
time: 188 us; the launch traced here: 187 us
  blocking collectives  145 us (77%)
  Pallas kernels  24 us (13%)
  starting transfers between devices  8.99 us (5%)
  waiting for transfers between devices  4.3 us (2%)
  local copies, waits for them, and re-layouts  3.98 us (2%)
    all_gather x2, blocking collectives, per_device(): gathered = lax.all_gather(block, NAMES, axis=0)  145 us
    pallas_call x3, Pallas kernels, run(): pl.pallas_call(functools.partial(body, names), out_shape=outs, in_specs=s...  24 us
    ppermute x6, starting transfers between devices, beside(): lax.ppermute(values, axis, [(i, (i + step) % count) for i in range(count)])  8.99 us
    ppermute x6, waiting for transfers between devices, beside(): lax.ppermute(values, axis, [(i, (i + step) % count) for i in range(count)])  4.3 us
  transfers between devices with their start and end apart: 6, of which 1 were waited for; matrix products, arithmetic and copies ran while one was open for 2% of the time, Pallas kernels for 1%

profile of v1, /device:TPU:0, one launch (start us, length us, event | category | flops | bytes accessed | tf_op | source)
XLA Modules:
  0.0 187.4 jit_solution(15139200176852748022)
XLA Ops:
  0.0 0.9 fusion.1
  0.9 3.1 %collective-permute-start.3 = (f32[16,1,128]{2,1,0:T(1,128)S(1)}, f32[16,1,128]{2,1,0:T(1,128)S(1)}, u32[]{:S(2)}, u32[]{:S(2)}) collective-permute-start(f32[16,1,128]{2,1,0:T(1,128)S(1)} %get-tuple-element.11), channel_id=1, source_target_pairs={{0,1},{1,0},{2,3},{3,2},{4,5},{5,4},{6,7},{7,6},{8,9},{9,8},{10,11... | collective-permute-start | bytes 24584 | tf_op jit(solution)/shard_map/ppermute | solution.py:363
  3.9 0.1 collective-permute-start.2
  4.0 0.7 fusion.2
  4.7 4.0 %collective-permute-start.1 = (f32[1,16,128]{2,1,0:T(8,128)S(1)}, f32[1,16,128]{2,1,0:T(8,128)S(1)}, u32[]{:S(2)}, u32[]{:S(2)}) collective-permute-start(f32[1,16,128]{2,1,0:T(8,128)S(1)} %get-tuple-element.13), channel_id=1, source_target_pairs={{0,24},{8,0},{16,8},{24,16},{1,25},{9,1},{17,9},{25,17},{2,26},{10... | collective-permute-start | bytes 24584 | tf_op jit(solution)/shard_map/ppermute | solution.py:363
  8.8 1.1 fusion
  9.8 0.1 copy.34
  10.0 0.0 collective-permute-start.5
  10.1 0.1 copy.33
  10.2 1.8 collective-permute-start.4
  12.0 2.1 %shard_map.208 = f32[4,8,128]{2,1,0:T(8,128)} custom-call(f32[64,128]{1,0:T(8,128)} %constant.40.clone.refs_0_.refs_3_, f32[128,128]{1,0:T(8,128)} %constant.41.clone.refs_1_, f32[128,128]{1,0:T(8,128)} %constant.42.clone.refs_2_, f32[16,16,128]{2,1,0:T(8,128)} %refs_13_.2), custom_call_target="tpu_custom_call" | custom-call | tf_op jit(solution)/shard_map/pallas_call | solution.py:386
  14.0 72.7 %all-gather = f32[128,8,128]{2,1,0:T(8,128)} all-gather(f32[4,8,128]{2,1,0:T(8,128)} %shard_map.208), channel_id=2, replica_groups=mesh['gx'=4,'gy'=4,'gz'=2] {'gx','gy','gz'}, dimensions={0}, use_global_device_ids=true | all-gather | bytes 540672 | tf_op jit(solution)/shard_map/all_gather | solution.py:418
  87.4 0.1 pad.1.clone
  87.5 0.0 collective-permute-done.4
  87.5 0.0 collective-permute-start
  87.5 0.2 copy.31
  87.7 0.0 collective-permute-done.5
  87.7 0.2 copy.32
  87.8 0.8 pad_maximum_fusion.refs_25_
  88.6 0.0 collective-permute-done.3.refs_24_
  88.6 0.0 copy-start
  88.6 0.0 collective-permute-done.2.refs_23_
  88.6 0.0 copy-start.1
  88.6 0.0 collective-permute-done.1.refs_22_
  88.6 0.0 copy-start.2
  88.6 4.3 %collective-permute-done.refs_21_ = f32[1,16,128]{2,1,0:T(8,128)S(1)} collective-permute-done((f32[1,16,128]{2,1,0:T(8,128)S(1)}, f32[1,16,128]{2,1,0:T(8,128)S(1)}, u32[]{:S(2)}, u32[]{:S(2)}) %collective-permute-start) | collective-permute-done | bytes 8224 | tf_op jit(solution)/shard_map/ppermute | solution.py:363
  92.9 0.0 copy-start.3
  92.9 0.0 copy-done
  92.9 0.0 copy-done.1
  92.9 0.0 copy-done.2
  92.9 0.6 copy-done.3
  93.5 13.8 %shard_map.209 = (f32[4,8,128]{2,1,0:T(8,128)}, f32[18,32,256]{2,1,0:T(8,128)}) custom-call(f32[64,128]{1,0:T(8,128)} %constant.40.clone.refs_0_.refs_3_, f32[128,128]{1,0:T(8,128)} %constant.41.clone.refs_1_, f32[128,128]{1,0:T(8,128)} %constant.42.clone.refs_2_, f32[64,128]{1,0:T(8,128)} %constant.40.clone.refs_0_.refs_3_, ...), custom_call_target="tpu_custom_call" | custom-call | tf_op jit(solution)/shard_map/pallas_call | solution.py:386
  107.3 71.9 %all-gather.1 = f32[128,8,128]{2,1,0:T(8,128)} all-gather(f32[4,8,128]{2,1,0:T(8,128)} %get-tuple-element.7), channel_id=3, replica_groups=mesh['gx'=4,'gy'=4,'gz'=2] {'gx','gy','gz'}, dimensions={0}, use_global_device_ids=true | all-gather | bytes 540672 | tf_op jit(solution)/shard_map/all_gather | solution.py:427
  179.3 8.1 %shard_map.210 = f32[16,16,128]{2,1,0:T(8,128)} custom-call(f32[64,128]{1,0:T(8,128)} %constant.40.clone.refs_0_.refs_3_, f32[256,128]{1,0:T(8,128)} %constant.43.clone.refs_4_.refs_1_, f32[32,128]{1,0:T(8,128)} %constant.44.clone.refs_5_.refs_2_, f32[128,64]{1,0:T(8,128)} %constant.45.clone.refs_6_.refs_3_, f32[32,64]{1,0:T(8,128)} %constant.46.clone.refs_7_.refs_4_, ...), custom_call_target="tpu_custom_call" | custom-call | tf_op jit(solution)/shard_map/pallas_call | solution.py:386
  (1 shorter events, 0.0 us)
Async XLA Ops:
  0.9 87.7 %collective-permute-start.3 = (f32[16,1,128]{2,1,0:T(1,128)S(1)}, f32[16,1,128]{2,1,0:T(1,128)S(1)}, u32[]{:S(2)}, u32[]{:S(2)}) collective-permute-start(f32[16,1,128]{2,1,0:T(1,128)S(1)} %get-tuple-element.11), channel_id=1, source_target_pairs={{0,1},{1,0},{2,3},{3,2},{4,5},{5,4},{6,7},{7,6},{8,9},{9,8},{10,11... | collective-permute-start | bytes 24584 | tf_op jit(solution)/shard_map/ppermute | solution.py:363
  3.9 84.6 %collective-permute-start.2 = (f32[16,1,128]{2,1,0:T(1,128)S(1)}, f32[16,1,128]{2,1,0:T(1,128)S(1)}, u32[]{:S(2)}, u32[]{:S(2)}) collective-permute-start(f32[16,1,128]{2,1,0:T(1,128)S(1)} %get-tuple-element.12), channel_id=1, source_target_pairs={{0,1},{1,0},{2,3},{3,2},{4,5},{5,4},{6,7},{7,6},{8,9},{9,8},{10,11... | collective-permute-start | bytes 24584 | tf_op jit(solution)/shard_map/ppermute | solution.py:363
  4.7 83.9 %collective-permute-start.1 = (f32[1,16,128]{2,1,0:T(8,128)S(1)}, f32[1,16,128]{2,1,0:T(8,128)S(1)}, u32[]{:S(2)}, u32[]{:S(2)}) collective-permute-start(f32[1,16,128]{2,1,0:T(8,128)S(1)} %get-tuple-element.13), channel_id=1, source_target_pairs={{0,24},{8,0},{16,8},{24,16},{1,25},{9,1},{17,9},{25,17},{2,26},{10... | collective-permute-start | bytes 24584 | tf_op jit(solution)/shard_map/ppermute | solution.py:363
  10.0 77.7 %collective-permute-start.5 = (f32[16,16]{1,0:T(8,128)S(1)}, f32[16,16]{1,0:T(8,128)S(1)}, u32[]{:S(2)}, u32[]{:S(2)}) collective-permute-start(f32[16,16]{1,0:T(8,128)S(1)} %bitcast.8), channel_id=1, source_target_pairs={{0,2},{2,4},{4,6},{6,0},{1,3},{3,5},{5,7},{7,1},{8,10},{10,12},{12... | collective-permute-start | bytes 3080 | tf_op jit(solution)/shard_map/ppermute | solution.py:363
  10.2 77.3 %collective-permute-start.4 = (f32[16,16]{1,0:T(8,128)S(1)}, f32[16,16]{1,0:T(8,128)S(1)}, u32[]{:S(2)}, u32[]{:S(2)}) collective-permute-start(f32[16,16]{1,0:T(8,128)S(1)} %bitcast.11), channel_id=1, source_target_pairs={{0,6},{2,0},{4,2},{6,4},{1,7},{3,1},{5,3},{7,5},{8,14},{10,8},{12,... | collective-permute-start | bytes 3080 | tf_op jit(solution)/shard_map/ppermute | solution.py:363
  87.5 5.5 %collective-permute-start = (f32[1,16,128]{2,1,0:T(8,128)S(1)}, f32[1,16,128]{2,1,0:T(8,128)S(1)}, u32[]{:S(2)}, u32[]{:S(2)}) collective-permute-start(f32[1,16,128]{2,1,0:T(8,128)S(1)} %get-tuple-element.14), channel_id=1, source_target_pairs={{0,8},{8,16},{16,24},{24,0},{1,9},{9,17},{17,25},{25,1},{2,10},{10... | collective-permute-start | bytes 24584 | tf_op jit(solution)/shard_map/ppermute | solution.py:363
  88.6 4.3 %copy-start = (f32[16,1,128]{2,1,0:T(1,128)}, f32[16,1,128]{2,1,0:T(1,128)S(1)}, u32[]{:S(2)}) copy-start(f32[16,1,128]{2,1,0:T(1,128)S(1)} %collective-permute-done.3.refs_24_) | copy-start | bytes 24580
  88.6 4.3 %copy-start.1 = (f32[16,1,128]{2,1,0:T(1,128)}, f32[16,1,128]{2,1,0:T(1,128)S(1)}, u32[]{:S(2)}) copy-start(f32[16,1,128]{2,1,0:T(1,128)S(1)} %collective-permute-done.2.refs_23_) | copy-start | bytes 24580
  88.6 4.3 %copy-start.2 = (f32[1,16,128]{2,1,0:T(8,128)}, f32[1,16,128]{2,1,0:T(8,128)S(1)}, u32[]{:S(2)}) copy-start(f32[1,16,128]{2,1,0:T(8,128)S(1)} %collective-permute-done.1.refs_22_) | copy-start | bytes 24580
  92.9 0.6 copy-start.3

commit v2 on v1

--- a/solution.py
+++ b/solution.py
@@ -17,6 +17,7 @@
 )
 LINEAR = ({-1: 0.25, 0: 0.75}, {0: 0.75, 1: 0.25})
 NAMES = ("gx", "gy", "gz")
+MESH = pl.DeviceIdType.MESH
 
 
 def basis(count):
@@ -274,31 +275,159 @@
     return center, f - (diagonal * center - weight * beside)
 
 
-def first_kernel(names, *refs):
+def position():
+    return tuple(lax.axis_index(name) for name in NAMES)
+
+
+def partner_of(place):
+    x, y, z = place
+    return (x, y + 1 - 2 * lax.rem(y, 2), z)
+
+
+def shifted(place, counts, offset):
+    return tuple(
+        lax.rem(at + step + count, count) for at, step, count in zip(place, offset, counts)
+    )
+
+
+def slot(place, counts):
+    return (place[0] * counts[1] + place[1]) * counts[2] + place[2]
+
+
+def chip_offsets(counts):
+    nx, ny, nz = counts
+    offsets = [
+        (dx, dy, dz) for dx in range(nx) for dy in range(0, ny, 2) for dz in range(nz)
+    ]
+
+    def hops(offset):
+        return sum(min(step, count - step) for step, count in zip(offset, (nx, ny, nz)))
+
+    return sorted(offsets[1:], key=hops, reverse=True)
+
+
+def face_offsets(counts):
+    faces = []
+    for axis in range(3):
+        for side, step in ((0, -1), (1, 1)):
+            offset = [0, 0, 0]
+            offset[axis] = step
+            faces.append((tuple(offset), axis, side))
+    return faces
+
+
+def greet(barrier, places):
+    for place in places:
+        pl.semaphore_signal(barrier, inc=1, device_id=place, device_id_type=MESH)
+
+
+def remote(src, dst, send, recv, place):
+    return pltpu.make_async_remote_copy(
+        src_ref=src, dst_ref=dst, send_sem=send, recv_sem=recv, device_id=place, device_id_type=MESH
+    )
+
+
+def spread(counts, block, gathered, sems):
+    send, recv, relay_send, relay_recv = sems
+    me = position()
+    partner = partner_of(me)
+    offsets = chip_offsets(counts)
+    mine = gathered.at[slot(me, counts)]
+    copies = []
+    for n, offset in enumerate(offsets):
+        place = shifted(me, counts, offset)
+        copies.append(remote(block, mine, send.at[n], recv.at[n], place))
+        copies[-1].start()
+    last = len(offsets)
+    relays = [remote(block, mine, relay_send.at[last], relay_recv.at[last], partner)]
+    relays[0].start()
+
+    def finish():
+        gathered[slot(me, counts)] = block[...]
+        for n, offset in reversed(list(enumerate(offsets))):
+            copies[n].wait_recv()
+            source = shifted(me, counts, tuple(-step for step in offset))
+            arrived = gathered.at[slot(source, counts)]
+            relays.append(
+                remote(arrived, arrived, relay_send.at[n], relay_recv.at[n], partner)
+            )
+            relays[-1].start()
+        for copy in copies:
+            copy.wait_send()
+        for relay in relays:
+            relay.wait()
+
+    return finish
+
+
+def gather_places(counts):
+    me = position()
+    return [shifted(me, counts, offset) for offset in chip_offsets(counts)] + [partner_of(me)]
+
+
+def first_kernel(names, counts, *refs):
     k = dict(zip(names, refs))
-    source, out = refs[len(names) :]
+    (source, gathered, planes, rows, columns) = refs[len(names) : len(names) + 5]
+    block, own_planes, own_rows, own_columns, *sems, face_send, face_recv = refs[len(names) + 5 :]
+    me = position()
+    barrier = pltpu.get_barrier_semaphore()
+    faces = face_offsets(counts)
+    places = gather_places(counts) + [shifted(me, counts, offset) for offset, _, _ in faces]
+    greet(barrier, places)
     b0, b1, b2 = source.shape
     summed = source[...].reshape(b0 // 2, 2, b1, b2)
-    out[...] = restrict_own(k, summed[:, 0] + summed[:, 1]).reshape(out.shape)
+    block[...] = restrict_own(k, summed[:, 0] + summed[:, 1]).reshape(block.shape)
+    own_planes[0] = source[0]
+    own_planes[1] = source[b0 - 1]
+    own_rows[0] = source[:, pl.ds(0, 1), :]
+    own_rows[1] = source[:, pl.ds(b1 - 1, 1), :]
+    turned = source[...].reshape(b0 * b1, b2).T
+    own_columns[0] = turned[:8]
+    own_columns[1] = turned[b2 - 8 :]
+    pl.semaphore_wait(barrier, len(places))
+    finish = spread(counts, block, gathered, sems)
+    buffers = ((own_planes, planes), (own_rows, rows), (own_columns, columns))
+    order = (0, 2, 1)
+    copies = []
+    for n, (offset, axis, side) in enumerate(faces):
+        own, halo = buffers[order[axis]]
+        place = shifted(me, counts, offset)
+        copies.append(
+            remote(own.at[side], halo.at[1 - side], face_send.at[n], face_recv.at[n], place)
+        )
+        copies[-1].start()
+    finish()
+    for copy in copies:
+        copy.wait()
+
+
+def gather_kernel(counts, block, gathered, *sems):
+    barrier = pltpu.get_barrier_semaphore()
+    places = gather_places(counts)
+    greet(barrier, places)
+    pl.semaphore_wait(barrier, len(places))
+    spread(counts, block, gathered, sems)()
 
 
 def second_kernel(names, counts, shape2, span, *refs):
     k = dict(zip(names, refs))
-    (shift_ref, gathered, source, plane_lo, plane_hi, row_lo, row_hi, lane_halo) = refs[
-        len(names) : len(names) + 8
+    (shift_ref, gathered, source, plane_halo, row_halo, column_halo) = refs[
+        len(names) : len(names) + 6
     ]
-    out, v1, g, v, u, t, z, zw, v0, f, summed = refs[len(names) + 8 :]
+    out, v1, g, v, u, t, z, zw, v0, f, summed = refs[len(names) + 6 :]
     shift = shift_ref[0]
     unpack(gathered, counts, g)
     b0, b1, b2 = source.shape
     f[...] = jnp.zeros_like(f)
     rows, lanes = pl.ds(8, b1), pl.ds(b2, b2)
     f[1 : b0 + 1, rows, lanes] = source[...]
-    f[0, rows, lanes] = plane_lo[0]
-    f[b0 + 1, rows, lanes] = plane_hi[0]
-    f[1 : b0 + 1, pl.ds(7, 1), lanes] = row_lo[...]
-    f[1 : b0 + 1, pl.ds(8 + b1, 1), lanes] = row_hi[...]
-    f[1 : b0 + 1, rows, pl.ds(0, b2)] = lane_halo[...]
+    f[0, rows, lanes] = plane_halo[0]
+    f[b0 + 1, rows, lanes] = plane_halo[1]
+    f[1 : b0 + 1, pl.ds(7, 1), lanes] = row_halo[0]
+    f[1 : b0 + 1, pl.ds(8 + b1, 1), lanes] = row_halo[1]
+    middle = jnp.zeros((b2 - 16, b0 * b1), jnp.float32)
+    turned = jnp.concatenate([column_halo[1], middle, column_halo[0]], axis=0)
+    f[1 : b0 + 1, rows, pl.ds(0, b2)] = turned.T.reshape(b0, b1, b2)
     def pair_sum(i):
         t[i] = g[2 * i] + g[2 * i + 1]
 
@@ -356,11 +485,6 @@
         out[p] = center + damp * rest
 
     loop(b0, after)
-
-
-def beside(values, axis, step):
-    count = lax.axis_size(axis)
-    return lax.ppermute(values, axis, [(i, (i + step) % count) for i in range(count)])
 
 
 def per_device(counts, source, shift):
@@ -374,12 +498,11 @@
     wide = (b1 + 16, 2 * b2)
     packed = jax.ShapeDtypeStruct((b0 // 4, b1 // 2, b2), jnp.float32)
     vmem = pl.BlockSpec(memory_space=pltpu.VMEM)
-    params = pltpu.CompilerParams(vmem_limit_bytes=60 * 1024 * 1024)
 
     def field(*shape):
         return pltpu.VMEM(shape, jnp.float32)
 
-    def run(body, names, operands, outs, scratch, smem):
+    def run(body, names, operands, outs, scratch, smem, collective=None):
         specs = [vmem] * len(names)
         specs += [pl.BlockSpec(memory_space=pltpu.SMEM)] * smem
         specs += [vmem] * (len(operands) - smem)
@@ -389,7 +512,11 @@
             in_specs=specs,
             out_specs=[vmem] * len(outs) if isinstance(outs, tuple) else vmem,
             scratch_shapes=scratch,
-            compiler_params=params,
+            compiler_params=pltpu.CompilerParams(
+                vmem_limit_bytes=60 * 1024 * 1024,
+                collective_id=collective,
+                has_side_effects=collective is not None,
+            ),
         )(*[jnp.asarray(table[name]) for name in names], *operands)
 
     own = ("own_rows", "own_lo", "own_hi")
@@ -397,15 +524,6 @@
     linear = tuple(name for name in table if name.startswith("linear"))
     linear_low = tuple(name for name in linear if not name.endswith("0"))
     cubic = tuple(name for name in table if name.startswith("cubic"))
-    plane_lo = beside(source[-1:], "gx", 1)
-    plane_hi = beside(source[:1], "gx", -1)
-    row_lo = beside(source[:, -1:], "gz", 1)
-    row_hi = beside(source[:, :1], "gz", -1)
-    lane_lo = beside(source[:, :, -1], "gy", 1)
-    lane_hi = beside(source[:, :, 0], "gy", -1)
-    lane_halo = jnp.concatenate(
-        [lane_hi[:, :, None], jnp.zeros((b0, b1, b2 - 2), jnp.float32), lane_lo[:, :, None]], axis=2
-    )
     buffers = [
         field(m0, m1, m2),
         field(m0 + 2, m1, m2),
@@ -414,17 +532,33 @@
         field(m0 // 2, m1, m2),
         field(span, *wide),
     ]
-    block = run(first_kernel, own, (source,), packed, [], 0)
-    gathered = lax.all_gather(block, NAMES, axis=0)
+    devices = nx * ny * nz
+    chips = devices // 2
+    sems = [pltpu.SemaphoreType.DMA((max(chips - 1, 1),))] * 2
+    sems += [pltpu.SemaphoreType.DMA((chips,))] * 2
+    everyone = jax.ShapeDtypeStruct((devices, *packed.shape), jnp.float32)
+    face_shapes = ((2, b1, b2), (2, b0, 1, b2), (2, 8, b0 * b1))
+    gathered, *halos = run(
+        lambda names, *refs: first_kernel(names, counts, *refs),
+        own,
+        (source,),
+        (everyone, *[jax.ShapeDtypeStruct(shape, jnp.float32) for shape in face_shapes]),
+        [field(*packed.shape), *[field(*shape) for shape in face_shapes], *sems]
+        + [pltpu.SemaphoreType.DMA((6,))] * 2,
+        0,
+        0,
+    )
     block, v1 = run(
         lambda names, *refs: second_kernel(names, counts, shape2, span, *refs),
         own + coarse + linear_low + cubic,
-        (shift, gathered, source, plane_lo, plane_hi, row_lo, row_hi, lane_halo),
+        (shift, gathered, source, *halos),
         (packed, jax.ShapeDtypeStruct((b0 + 2, *wide), jnp.float32)),
         buffers + [field(b0 + 4, *wide), field(b0 + 2, *wide), field(b0 // 2, b1, b2)],
         1,
     )
-    gathered = lax.all_gather(block, NAMES, axis=0)
+    gathered = run(
+        lambda names, *refs: gather_kernel(counts, *refs), (), (block,), everyone, sems, 0, 1
+    )
     return run(
         lambda names, *refs: third_kernel(names, counts, shape2, span, *refs),
         coarse + linear,

time: 188 us -> 52.7 us (0.28)
  blocking collectives: 145 us -> 0 us
  Pallas kernels: 24 us -> 51.8 us
  starting transfers between devices: 8.99 us -> 0 us
  waiting for transfers between devices: 4.3 us -> 0 us
  local copies, waits for them, and re-layouts: 3.98 us -> 0 us
    all_gather x2 -> x0, blocking collectives: 145 us -> none  [per_device(): gathered = lax.all_gather(block, NAMES, axis=0)]
    pallas_call x3 -> x4, Pallas kernels: 24 us -> 51.8 us  [run(): pl.pallas_call(functools.partial(body, names), out_shape=outs, in_specs=s...]
    ppermute x6 -> x0, starting transfers between devices: 8.99 us -> none  [beside(): lax.ppermute(values, axis, [(i, (i + step) % count) for i in range(count)])]
    ppermute x6 -> x0, waiting for transfers between devices: 4.3 us -> none  [beside(): lax.ppermute(values, axis, [(i, (i + step) % count) for i in range(count)])]
    slice x3 -> x0, local copies, waits for them, and re-layouts: 2.67 us -> none  [the longest x1 1.07 us: per_device(): lane_hi = beside(source[:, :, 0], 'gy', -1)]
  transfers between devices with their start and end apart: 6 -> 0, of which waited for: 1 -> 0; matrix products, arithmetic and copies ran while one was open for 2% -> 0% of each run, Pallas kernels for 1% -> 0%
where the time goes in v2:
time: 52.7 us; the launch traced here: 52.5 us
  Pallas kernels  51.8 us (98%)
  between operations  0.67 us (1%)
    pallas_call x4, Pallas kernels, run(): pl.pallas_call(functools.partial(body, names), out_shape=outs, in_specs=s...  51.8 us

profile of v2, /device:TPU:0, one launch (start us, length us, event | category | flops | bytes accessed | tf_op | source)
XLA Modules:
  0.0 52.5 jit_solution(605872095364089098)
XLA Ops:
  0.7 16.8 %shard_map.208 = (f32[32,4,8,128]{3,2,1,0:T(8,128)}, f32[2,16,128]{2,1,0:T(8,128)}, f32[2,16,1,128]{3,2,1,0:T(1,128)}, f32[2,8,256]{2,1,0:T(8,128)}) custom-call(f32[64,128]{1,0:T(8,128)} %constant.38.clone.refs_0_.refs_3_, f32[128,128]{1,0:T(8,128)} %constant.39.clone.refs_1_, f32[128,128]{1,0:T(8,128)} %constant.40.clone.refs_2_, f32[16,16,128]{2,1,0:T(8,128)} %refs_13_.2), custom_call_target="tpu_custom_call" | custom-call | tf_op jit(solution)/shard_map/pallas_call | solution.py:509
  17.5 13.9 %shard_map.209 = (f32[4,8,128]{2,1,0:T(8,128)}, f32[18,32,256]{2,1,0:T(8,128)}) custom-call(f32[64,128]{1,0:T(8,128)} %constant.38.clone.refs_0_.refs_3_, f32[128,128]{1,0:T(8,128)} %constant.39.clone.refs_1_, f32[128,128]{1,0:T(8,128)} %constant.40.clone.refs_2_, f32[64,128]{1,0:T(8,128)} %constant.38.clone.refs_0_.refs_3_, ...), custom_call_target="tpu_custom_call" | custom-call | tf_op jit(solution)/shard_map/pallas_call | solution.py:509
  31.4 13.0 %shard_map.210.refs_12_ = f32[32,4,8,128]{3,2,1,0:T(8,128)} custom-call(f32[4,8,128]{2,1,0:T(8,128)} %get-tuple-element.15.refs_0_), custom_call_target="tpu_custom_call" | custom-call | tf_op jit(solution)/shard_map/pallas_call | solution.py:509
  44.3 8.1 %shard_map.211 = f32[16,16,128]{2,1,0:T(8,128)} custom-call(f32[64,128]{1,0:T(8,128)} %constant.38.clone.refs_0_.refs_3_, f32[256,128]{1,0:T(8,128)} %constant.41.clone.refs_4_.refs_1_, f32[32,128]{1,0:T(8,128)} %constant.42.clone.refs_5_.refs_2_, f32[128,64]{1,0:T(8,128)} %constant.43.clone.refs_6_.refs_3_, f32[32,64]{1,0:T(8,128)} %constant.44.clone.refs_7_.refs_4_, ...), custom_call_target="tpu_custom_call" | custom-call | tf_op jit(solution)/shard_map/pallas_call | solution.py:509

commit v3 on v2

--- a/solution.py
+++ b/solution.py
@@ -84,11 +84,42 @@
         - two * cos2[None, None, :]
     )
     table["eigen"] = (np.float32(0.25 ** (LEVELS - 1)) * eigen).reshape(c0 * c1, c2)
-    return {name: np.asarray(value, np.float32) for name, value in table.items()}
+    wide = ("spectrum_rows", "spectrum_lanes", "eigen")
+    return {
+        name: np.asarray(
+            value, np.float32 if name in wide or name.endswith("2") else jnp.bfloat16
+        )
+        for name, value in table.items()
+    }
 
 
 def dot(a, b):
     return jnp.dot(a, b, precision=PRECISE, preferred_element_type=jnp.float32)
+
+
+def parts_of(values, pieces):
+    parts = []
+    for n in range(pieces):
+        parts.append(values.astype(jnp.bfloat16))
+        if n + 1 < pieces:
+            values = values - parts[-1].astype(jnp.float32)
+    return parts[::-1]
+
+
+def right(values, matrix, pieces):
+    terms = [
+        jnp.dot(part, matrix, preferred_element_type=jnp.float32)
+        for part in parts_of(values, pieces)
+    ]
+    return sum(terms[1:], terms[0])
+
+
+def left(matrix, values, pieces):
+    terms = [
+        jnp.dot(matrix, part, preferred_element_type=jnp.float32)
+        for part in parts_of(values, pieces)
+    ]
+    return sum(terms[1:], terms[0])
 
 
 def around(plane):
@@ -106,10 +137,10 @@
     return first
 
 
-def row_blocks(matrix, values):
+def row_blocks(matrix, values, pieces):
     depth = matrix.shape[1]
     return jnp.concatenate(
-        [dot(matrix, values[i : i + depth]) for i in range(0, values.shape[0], depth)], axis=0
+        [left(matrix, values[i : i + depth], pieces) for i in range(0, values.shape[0], depth)], axis=0
     )
 
 
@@ -135,9 +166,9 @@
 
 def restrict_own(k, summed):
     b_half, rows, lanes = summed.shape
-    folded = dot(k["own_rows"][...], summed.reshape(b_half * rows, lanes))
+    folded = left(k["own_rows"][...], summed.reshape(b_half * rows, lanes), 3)
     half = folded.shape[0] // 2
-    return dot(folded[:half], k["own_lo"][...]) + dot(folded[half:], k["own_hi"][...])
+    return right(folded[:half], k["own_lo"][...], 3) + right(folded[half:], k["own_hi"][...], 3)
 
 
 def unpack(gathered, counts, g):
@@ -181,13 +212,13 @@
 
 
 def down(k, t, shape2):
-    flat = row_blocks(k["down_rows"][...], t[...].reshape(-1, t.shape[2]))
-    return dot(flat, k["down_lanes"][...]).reshape(shape2)
+    flat = row_blocks(k["down_rows"][...], t[...].reshape(-1, t.shape[2]), 3)
+    return right(flat, k["down_lanes"][...], 3).reshape(shape2)
 
 
 def up(k, kind, level, values, z):
-    flat = dot(values, k[kind + "_lanes" + level][...])
-    z[...] = row_blocks(k[kind + "_rows" + level][...], flat).reshape(z.shape)
+    flat = right(values, k[kind + "_lanes" + level][...], 2)
+    z[...] = row_blocks(k[kind + "_rows" + level][...], flat, 2).reshape(z.shape)
 
 
 def blend(z, i, weights, count):
@@ -365,10 +396,10 @@
     return [shifted(me, counts, offset) for offset in chip_offsets(counts)] + [partner_of(me)]
 
 
-def first_kernel(names, counts, *refs):
-    k = dict(zip(names, refs))
-    (source, gathered, planes, rows, columns) = refs[len(names) : len(names) + 5]
-    block, own_planes, own_rows, own_columns, *sems, face_send, face_recv = refs[len(names) + 5 :]
+def first_part(k, counts, source, f, gathered, halos, block, owns, sems, face_sems):
+    own_planes, own_rows, own_columns = owns
+    planes, rows, columns = halos
+    face_send, face_recv = face_sems
     me = position()
     barrier = pltpu.get_barrier_semaphore()
     faces = face_offsets(counts)
@@ -396,31 +427,19 @@
             remote(own.at[side], halo.at[1 - side], face_send.at[n], face_recv.at[n], place)
         )
         copies[-1].start()
+    f[...] = jnp.zeros_like(f)
+    f[1 : b0 + 1, pl.ds(8, b1), pl.ds(b2, b2)] = source[...]
     finish()
     for copy in copies:
         copy.wait()
 
 
-def gather_kernel(counts, block, gathered, *sems):
-    barrier = pltpu.get_barrier_semaphore()
-    places = gather_places(counts)
-    greet(barrier, places)
-    pl.semaphore_wait(barrier, len(places))
-    spread(counts, block, gathered, sems)()
-
-
-def second_kernel(names, counts, shape2, span, *refs):
-    k = dict(zip(names, refs))
-    (shift_ref, gathered, source, plane_halo, row_halo, column_halo) = refs[
-        len(names) : len(names) + 6
-    ]
-    out, v1, g, v, u, t, z, zw, v0, f, summed = refs[len(names) + 6 :]
-    shift = shift_ref[0]
+def second_part(k, counts, shape2, span, shift, gathered, source, halos, out, buffers):
+    g, v, u, t, z, zw, v0, v1, f, summed = buffers
+    plane_halo, row_halo, column_halo = halos
     unpack(gathered, counts, g)
     b0, b1, b2 = source.shape
-    f[...] = jnp.zeros_like(f)
     rows, lanes = pl.ds(8, b1), pl.ds(b2, b2)
-    f[1 : b0 + 1, rows, lanes] = source[...]
     f[0, rows, lanes] = plane_halo[0]
     f[b0 + 1, rows, lanes] = plane_halo[1]
     f[1 : b0 + 1, pl.ds(7, 1), lanes] = row_halo[0]
@@ -460,10 +479,8 @@
     out[...] = restrict_own(k, summed[...]).reshape(out.shape)
 
 
-def third_kernel(names, counts, shape2, span, *refs):
-    k = dict(zip(names, refs))
-    shift_ref, gathered, source, v1, out, g, v, u, t, z, zw, w = refs[len(names) :]
-    shift = shift_ref[0]
+def third_part(k, counts, shape2, span, shift, gathered, source, out, buffers):
+    g, v, u, t, z, zw, w, v1 = buffers[:8]
     unpack(gathered, counts, g)
     cycle1(k, v, u, g, t, z, shift, True, shape2)
     b0 = source.shape[0]
@@ -485,6 +502,21 @@
         out[p] = center + damp * rest
 
     loop(b0, after)
+
+
+def kernel(names, counts, shape2, span, *refs):
+    k = dict(zip(names, refs))
+    shift_ref, source, out, *rest = refs[len(names) :]
+    shift = shift_ref[0]
+    landing, later, *halos = rest[:5]
+    block, block_later, *owns = rest[5:10]
+    buffers = rest[10:20]
+    sems, sems_later, face_sems = rest[20:24], rest[24:28], rest[28:30]
+    f = buffers[8]
+    first_part(k, counts, source, f, landing, halos, block, owns, sems, face_sems)
+    second_part(k, counts, shape2, span, shift, landing, source, halos, block_later, buffers)
+    spread(counts, block_later, later, sems_later)()
+    third_part(k, counts, shape2, span, shift, later, source, out, buffers)
 
 
 def per_device(counts, source, shift):
@@ -496,34 +528,15 @@
     shape2 = tuple(size // 4 for size in sizes)
     span = b0 // 2 + 8
     wide = (b1 + 16, 2 * b2)
-    packed = jax.ShapeDtypeStruct((b0 // 4, b1 // 2, b2), jnp.float32)
+    packed = (b0 // 4, b1 // 2, b2)
+    devices = nx * ny * nz
+    chips = devices // 2
     vmem = pl.BlockSpec(memory_space=pltpu.VMEM)
 
     def field(*shape):
         return pltpu.VMEM(shape, jnp.float32)
 
-    def run(body, names, operands, outs, scratch, smem, collective=None):
-        specs = [vmem] * len(names)
-        specs += [pl.BlockSpec(memory_space=pltpu.SMEM)] * smem
-        specs += [vmem] * (len(operands) - smem)
-        return pl.pallas_call(
-            functools.partial(body, names),
-            out_shape=outs,
-            in_specs=specs,
-            out_specs=[vmem] * len(outs) if isinstance(outs, tuple) else vmem,
-            scratch_shapes=scratch,
-            compiler_params=pltpu.CompilerParams(
-                vmem_limit_bytes=60 * 1024 * 1024,
-                collective_id=collective,
-                has_side_effects=collective is not None,
-            ),
-        )(*[jnp.asarray(table[name]) for name in names], *operands)
-
-    own = ("own_rows", "own_lo", "own_hi")
-    coarse = ("down_rows", "down_lanes", "spectrum_rows", "spectrum_lanes", "eigen")
-    linear = tuple(name for name in table if name.startswith("linear"))
-    linear_low = tuple(name for name in linear if not name.endswith("0"))
-    cubic = tuple(name for name in table if name.startswith("cubic"))
+    faces = [field(2, b1, b2), field(2, b0, 1, b2), field(2, 8, b0 * b1)]
     buffers = [
         field(m0, m1, m2),
         field(m0 + 2, m1, m2),
@@ -531,42 +544,30 @@
         field(m0 // 2, m1, m2),
         field(m0 // 2, m1, m2),
         field(span, *wide),
+        field(b0 + 4, *wide),
+        field(b0 + 2, *wide),
+        field(b0 + 2, *wide),
+        field(b0 // 2, b1, b2),
     ]
-    devices = nx * ny * nz
-    chips = devices // 2
     sems = [pltpu.SemaphoreType.DMA((max(chips - 1, 1),))] * 2
     sems += [pltpu.SemaphoreType.DMA((chips,))] * 2
-    everyone = jax.ShapeDtypeStruct((devices, *packed.shape), jnp.float32)
-    face_shapes = ((2, b1, b2), (2, b0, 1, b2), (2, 8, b0 * b1))
-    gathered, *halos = run(
-        lambda names, *refs: first_kernel(names, counts, *refs),
-        own,
-        (source,),
-        (everyone, *[jax.ShapeDtypeStruct(shape, jnp.float32) for shape in face_shapes]),
-        [field(*packed.shape), *[field(*shape) for shape in face_shapes], *sems]
+    landing = [field(devices, *packed)] * 2 + faces
+    names = tuple(table)
+    return pl.pallas_call(
+        functools.partial(kernel, names, counts, shape2, span),
+        out_shape=jax.ShapeDtypeStruct(source.shape, jnp.float32),
+        in_specs=[vmem] * len(names) + [pl.BlockSpec(memory_space=pltpu.SMEM), vmem],
+        out_specs=vmem,
+        scratch_shapes=landing
+        + [field(*packed)] * 2
+        + faces
+        + buffers
+        + sems * 2
         + [pltpu.SemaphoreType.DMA((6,))] * 2,
-        0,
-        0,
-    )
-    block, v1 = run(
-        lambda names, *refs: second_kernel(names, counts, shape2, span, *refs),
-        own + coarse + linear_low + cubic,
-        (shift, gathered, source, *halos),
-        (packed, jax.ShapeDtypeStruct((b0 + 2, *wide), jnp.float32)),
-        buffers + [field(b0 + 4, *wide), field(b0 + 2, *wide), field(b0 // 2, b1, b2)],
-        1,
-    )
-    gathered = run(
-        lambda names, *refs: gather_kernel(counts, *refs), (), (block,), everyone, sems, 0, 1
-    )
-    return run(
-        lambda names, *refs: third_kernel(names, counts, shape2, span, *refs),
-        coarse + linear,
-        (shift, gathered, source, v1),
-        jax.ShapeDtypeStruct(source.shape, jnp.float32),
-        buffers + [field(b0 + 4, *wide)],
-        1,
-    )
+        compiler_params=pltpu.CompilerParams(
+            vmem_limit_bytes=60 * 1024 * 1024, collective_id=0, has_side_effects=True
+        ),
+    )(*[jnp.asarray(table[name]) for name in names], shift, source)
 
 
 def solution(mesh):

time: 52.7 us -> 44.1 us (0.84)
  Pallas kernels: 51.8 us -> 41.7 us
  local copies, waits for them, and re-layouts: 0 us -> 1.57 us
    pallas_call x4 -> x1, Pallas kernels: 51.8 us -> 41.7 us  [per_device(): pl.pallas_call(functools.partial(kernel, names, counts, shape2, span), ou...]
    unnamed x0 -> x1, local copies, waits for them, and re-layouts: none -> 1.57 us
where the time goes in v3:
time: 44.1 us; the launch traced here: 44 us
  Pallas kernels  41.7 us (95%)
  local copies, waits for them, and re-layouts  1.57 us (4%)
  between operations  0.66 us (1%)
    pallas_call x1, Pallas kernels, per_device(): pl.pallas_call(functools.partial(kernel, names, counts, shape2, span), ou...  41.7 us
    unnamed x1, local copies, waits for them, and re-layouts  1.57 us

profile of v3, /device:TPU:0, one launch (start us, length us, event | category | flops | bytes accessed | tf_op | source)
XLA Modules:
  0.0 44.0 jit_solution(17601407406390009572)
XLA Ops:
  0.7 41.7 %shard_map.208 = f32[16,16,128]{2,1,0:T(8,128)} custom-call(bf16[64,128]{1,0:T(8,128)(2,1)} %constant.38.clone.refs_0_.refs_3_, bf16[128,128]{1,0:T(8,128)(2,1)} %constant.39.clone.refs_1_, bf16[128,128]{1,0:T(8,128)(2,1)} %constant.40.clone.refs_2_, bf16[64,128]{1,0:T(8,128)(2,1)} %constant.38.clone.refs_0_.refs_3_, ...), custom_call_target="tpu_custom_call" | custom-call | tf_op jit(solution)/shard_map/pallas_call | solution.py:556
  42.4 1.6 %copy.25 = f32[16,16,128]{2,1,0:T(8,128)} copy(f32[16,16,128]{2,1,0:T(8,128)} %shard_map.208) | data formatting | bytes 262144

commit v4 on v3

--- a/solution.py
+++ b/solution.py
@@ -362,38 +362,61 @@
     send, recv, relay_send, relay_recv = sems
     me = position()
     partner = partner_of(me)
-    offsets = chip_offsets(counts)
+    along, across = stages(counts)
+    number = {offset: n for n, offset in enumerate(chip_offsets(counts))}
     mine = gathered.at[slot(me, counts)]
-    copies = []
-    for n, offset in enumerate(offsets):
-        place = shifted(me, counts, offset)
-        copies.append(remote(block, mine, send.at[n], recv.at[n], place))
-        copies[-1].start()
-    last = len(offsets)
-    relays = [remote(block, mine, relay_send.at[last], relay_recv.at[last], partner)]
-    relays[0].start()
+    copies, relays = {}, []
+
+    def pass_on(offset, source, target, place):
+        n = number[offset]
+        copies[offset] = remote(source, target, send.at[n], recv.at[n], place)
+        copies[offset].start()
+
+    def relay(n, source, target):
+        relays.append(remote(source, target, relay_send.at[n], relay_recv.at[n], partner))
+        relays[-1].start()
+
+    for offset in along + across:
+        pass_on(offset, block, mine, shifted(me, counts, offset))
+    relay(len(number), block, mine)
+
+    def arrival(offset):
+        copies[offset].wait_recv()
+        source = shifted(me, counts, tuple(-step for step in offset))
+        return gathered.at[slot(source, counts)]
 
     def finish():
         gathered[slot(me, counts)] = block[...]
-        for n, offset in reversed(list(enumerate(offsets))):
-            copies[n].wait_recv()
-            source = shifted(me, counts, tuple(-step for step in offset))
-            arrived = gathered.at[slot(source, counts)]
-            relays.append(
-                remote(arrived, arrived, relay_send.at[n], relay_recv.at[n], partner)
-            )
-            relays[-1].start()
-        for copy in copies:
+        for first in along[::-1]:
+            arrived = arrival(first)
+            for second in across:
+                place = shifted(me, counts, second)
+                pass_on((first[0], second[1], second[2]), arrived, arrived, place)
+            relay(number[first], arrived, arrived)
+        for first in ((0, 0, 0), *along[::-1]):
+            for second in across[::-1]:
+                offset = (first[0], second[1], second[2])
+                arrived = arrival(offset)
+                relay(number[offset], arrived, arrived)
+        for copy in copies.values():
             copy.wait_send()
-        for relay in relays:
-            relay.wait()
+        for copy in relays:
+            copy.wait()
 
     return finish
+
+
+def stages(counts):
+    offsets = chip_offsets(counts)
+    along = [offset for offset in offsets if offset[1:] == (0, 0)]
+    across = [offset for offset in offsets if offset[0] == 0]
+    return along, across
 
 
 def gather_places(counts):
     me = position()
-    return [shifted(me, counts, offset) for offset in chip_offsets(counts)] + [partner_of(me)]
+    along, across = stages(counts)
+    return [shifted(me, counts, offset) for offset in along + across] + [partner_of(me)]
 
 
 def first_part(k, counts, source, f, gathered, halos, block, owns, sems, face_sems):

time: 44.1 us -> 42.9 us (0.973)
  Pallas kernels: 41.7 us -> 40.5 us
    pallas_call x1, Pallas kernels: 41.7 us -> 40.5 us  [per_device(): pl.pallas_call(functools.partial(kernel, names, counts, shape2, span), ou...]
where the time goes in v4:
time: 42.9 us; the launch traced here: 42.7 us
  Pallas kernels  40.5 us (94%)
  local copies, waits for them, and re-layouts  1.57 us (4%)
  between operations  0.66 us (2%)
    pallas_call x1, Pallas kernels, per_device(): pl.pallas_call(functools.partial(kernel, names, counts, shape2, span), ou...  40.5 us
    unnamed x1, local copies, waits for them, and re-layouts  1.57 us

profile of v4, /device:TPU:0, one launch (start us, length us, event | category | flops | bytes accessed | tf_op | source)
XLA Modules:
  0.0 42.7 jit_solution(17750925807923673722)
XLA Ops:
  0.7 40.5 %shard_map.208 = f32[16,16,128]{2,1,0:T(8,128)} custom-call(bf16[64,128]{1,0:T(8,128)(2,1)} %constant.38.clone.refs_0_.refs_3_, bf16[128,128]{1,0:T(8,128)(2,1)} %constant.39.clone.refs_1_, bf16[128,128]{1,0:T(8,128)(2,1)} %constant.40.clone.refs_2_, bf16[64,128]{1,0:T(8,128)(2,1)} %constant.38.clone.refs_0_.refs_3_, ...), custom_call_target="tpu_custom_call" | custom-call | tf_op jit(solution)/shard_map/pallas_call | solution.py:579
  41.1 1.6 %copy.25 = f32[16,16,128]{2,1,0:T(8,128)} copy(f32[16,16,128]{2,1,0:T(8,128)} %shard_map.208) | data formatting | bytes 262144
